TPU v7x, 32 devices: a whole 2x2x4 slice. The times are simulated.
32 devices in a mesh: dp: 4 (over z), mp: 8 (over y, x, core).
Axes of the slice: x: 2, y: 2, z: 4, core: 2. Of those that a mesh axis runs over, the one named last changes fastest.
Arguments:
- inputs: bfloat16 [197, 49152], P(None, ('dp', 'mp')), may hold values from -6 to 6
- cotangent: bfloat16 [197, 49152], P(None, ('dp', 'mp')), may hold values from -1.1953125 to 1.1953125
- w_in: bfloat16 [768, 3072], P('dp', 'mp'), may hold values from -0.21875 to 0.21875
- w_out: bfloat16 [3072, 768], P('mp', 'dp'), may hold values from -0.109375 to 0.109375
- prec_in: float32 [768, 3072], P('dp', 'mp'), may hold values from 0.1 to 2
- prec_out: float32 [3072, 768], P('mp', 'dp'), may hold values from 0.1 to 2
Outputs:
- new_prec_in: float32 [768, 3072], P('dp', 'mp')
- new_prec_out: float32 [3072, 768], P('mp', 'dp')
- new_w_in: float32 [768, 3072], P('dp', 'mp')
- new_w_out: float32 [3072, 768], P('mp', 'dp')
All inputs are finite; a program needn't handle non-finite values.
Results may differ from a plain program's by a relative error of at most 0.0028.
Values may be sent and summed in bfloat16 or wider, within the bound.
A program may use at most 64 MiB of HBM per device.

v0:
```python
import jax
import jax.numpy as jnp
from jax import lax
from jax.sharding import PartitionSpec as P

D = 768
SEQ = 197


def gelu_tanh(v):
    return jax.nn.gelu(v, approximate=True)


def per_device(inputs, cotangent, w_in, w_out, prec_in, prec_out):
    w_in_full, w_out_full = (
        lax.all_gather(w_in, "dp", axis=0, tiled=True),
        lax.all_gather(w_out, "dp", axis=1, tiled=True),
    )
    whole = lax.all_gather(inputs, "mp", axis=1, tiled=True)
    rows3 = whole.reshape(SEQ, -1, D)
    images = rows3.shape[1]
    pre = jnp.einsum("snd,dh->snh", rows3, w_in_full, preferred_element_type=jnp.float32)
    act = gelu_tanh(pre).astype(jnp.bfloat16)
    cot_whole = lax.all_gather(cotangent, "mp", axis=1, tiled=True)
    cot3 = cot_whole.reshape(SEQ, images, D)
    back = jnp.einsum("snd,hd->snh", cot3, w_out_full, preferred_element_type=jnp.float32)
    per_out = jnp.einsum("snh,snd->nhd", act, cot3, preferred_element_type=jnp.float32)
    sum_out = jnp.sum(per_out, 0)
    sq_out = jnp.sum(per_out * per_out, 0)
    delta = jax.vjp(gelu_tanh, pre)[1](back)[0].astype(jnp.bfloat16)
    rows_again = lax.all_gather(inputs, "mp", axis=1, tiled=True).reshape(SEQ, images, D)
    per_in = jnp.einsum("snd,snh->ndh", rows_again, delta, preferred_element_type=jnp.float32)
    sum_in = jnp.sum(per_in, 0)
    sq_in = jnp.sum(per_in * per_in, 0)
    sum_in, sq_in = (
        lax.psum_scatter(sum_in, "dp", scatter_dimension=0, tiled=True),
        lax.psum_scatter(sq_in, "dp", scatter_dimension=0, tiled=True),
    )
    sum_out, sq_out = (
        lax.psum_scatter(sum_out, "dp", scatter_dimension=1, tiled=True),
        lax.psum_scatter(sq_out, "dp", scatter_dimension=1, tiled=True),
    )
    scale = 1.0 / (images * lax.axis_size("dp"))
    new_prec_in = 0.6 * prec_in + 0.4 * sq_in * scale
    new_prec_out = 0.6 * prec_out + 0.4 * sq_out * scale
    w_in_own = w_in.astype(jnp.float32)
    w_out_own = w_out.astype(jnp.float32)
    new_w_in = w_in_own - 1.0 * (sum_in * scale + 0.1 * w_in_own) / (new_prec_in + 0.1)
    new_w_out = w_out_own - 1.0 * (sum_out * scale + 0.1 * w_out_own) / (new_prec_out + 0.1)
    return (new_prec_in, new_prec_out, new_w_in, new_w_out)


def solution(mesh):
    placed = (
        P(None, ("dp", "mp")),
        P(None, ("dp", "mp")),
        P("dp", "mp"),
        P("mp", "dp"),
        P("dp", "mp"),
        P("mp", "dp"),
    )
    return jax.shard_map(
        per_device,
        mesh=mesh,
        in_specs=placed,
        out_specs=(P("dp", "mp"), P("mp", "dp"), P("dp", "mp"), P("mp", "dp")),
        check_vma=False,
    )
```

profile of v0, /device:TPU:17, one launch (start us, length us, event | category | flops | bytes accessed | tf_op | source)
XLA Modules:
  0.0 241.6 jit_solution(8754437066115192813)
XLA Ops:
  8.7 13.8 %all_gather.16 = bf16[768,384]{1,0:T(8,128)(2,1)S(1)} all-gather(bf16[192,384]{1,0:T(8,128)(2,1)} %param.8), channel_id=1, replica_groups=mesh['dp'=4,'mp'=8] {'dp'}, dimensions={0}, use_global_device_ids=true | all-gather | bytes 737280 | tf_op jit(solution)/shard_map/all_gather | solution.py:16
  22.4 11.8 %all_gather.14 = bf16[384,768]{0,1:T(8,128)(2,1)S(1)} all-gather(bf16[384,192]{0,1:T(8,128)(2,1)} %param.9), channel_id=1, replica_groups=mesh['dp'=4,'mp'=8] {'dp'}, dimensions={1}, use_global_device_ids=true | all-gather | bytes 737280 | tf_op jit(solution)/shard_map/all_gather | solution.py:17
  34.3 16.7 %all-gather.5.cloned.1.call-done = bf16[197,12288]{1,0:T(8,128)(2,1)} async-done(((bf16[197,1536]{1,0:T(8,128)(2,1)}), bf16[197,12288]{1,0:T(8,128)(2,1)}) %all-gather.5.cloned.1.call-update) | async-done | bytes 4841488 | tf_op jit(solution)/shard_map/all_gather | solution.py:31
  51.0 3.8 %copy.47 = bf16[25,8,16,768]{3,2,1,0:T(8,128)(2,1)S(1)} copy(bf16[25,8,16,768]{3,1,2,0:T(8,128)(2,1)} %bitcast.30) | data formatting | bytes 9830400
  54.8 2.5 %slice.1 = bf16[197,16,768]{2,1,0:T(8,128)(2,1)} slice(bf16[200,16,768]{2,1,0:T(8,128)(2,1)S(1)} %bitcast.27), slice={[0:197], [0:16], [0:768]} | slice | bytes 9682944 | tf_op jit(solution)/shard_map/reshape | solution.py:31
  57.3 5.6 %multiply_convert_fusion = (bf16[197,16,384]{2,1,0:T(8,128)(2,1)}, f32[197,16,384]{2,1,0:T(8,128)}) fusion(bf16[768,384]{1,0:T(8,128)(2,1)S(1)} %all_gather.16, bf16[200,16,768]{2,1,0:T(8,128)(2,1)S(1)} %bitcast.28), kind=kOutput, calls=%fused_computation.17 | convolution fusion | flops 1870018560 | bytes 12693504 | tf_op jit(solution)/shard_map/snd,dh->snh/dot_general | solution.py:22
  62.9 29.6 %all-gather.3.cloned.1.call-done = bf16[197,12288]{1,0:T(8,128)(2,1)} async-done(((bf16[197,1536]{1,0:T(8,128)(2,1)}), bf16[197,12288]{1,0:T(8,128)(2,1)}) %all-gather.3.cloned.1.call-update) | async-done | bytes 4841488 | tf_op jit(solution)/shard_map/all_gather | solution.py:24
  92.5 3.9 %copy.46 = bf16[25,8,16,768]{3,2,1,0:T(8,128)(2,1)S(1)} copy(bf16[25,8,16,768]{3,1,2,0:T(8,128)(2,1)} %bitcast.29) | data formatting | bytes 9830400
  96.5 2.2 copy-done
  98.7 5.4 %fusion.11 = bf16[197,16,384]{2,1,0:T(8,128)(2,1)S(1)} fusion(f32[197,16,384]{2,1,0:T(8,128)S(1)} %copy-done.5, bf16[384,768]{0,1:T(8,128)(2,1)S(1)} %all_gather.14, bf16[200,16,768]{2,1,0:T(8,128)(2,1)S(1)} %bitcast.25), kind=kOutput, calls=%fused_computation.16 | convolution fusion | flops 1883332608 | bytes 12693504 | tf_op jit(solution)/shard_map/snd,hd->snh/dot_general | solution.py:26
  104.1 8.2 %bitcast_reduce_fusion = (f32[768,384]{0,1:T(8,128)S(1)}, f32[768,384]{0,1:T(8,128)S(1)}) fusion(bf16[197,16,768]{2,1,0:T(8,128)(2,1)S(1)} %bitcast.32, bf16[197,16,384]{2,1,0:T(8,128)(2,1)S(1)} %fusion.11), kind=kOutput, calls=%fused_computation | convolution fusion | flops 1872691200 | bytes 9621504 | tf_op jit(solution)/shard_map/snd,snh->ndh/dot_general | solution.py:32
  112.3 1.4 copy.38
  113.8 1.4 copy.42
  115.5 2.8 %slice = bf16[197,16,768]{2,1,0:T(8,128)(2,1)S(1)} slice(bf16[200,16,768]{2,1,0:T(8,128)(2,1)} %bitcast.26), slice={[0:197], [0:16], [0:768]} | slice | bytes 9682944 | tf_op jit(solution)/shard_map/reshape | solution.py:25
  118.6 8.2 %fusion.23 = (f32[384,768]{1,0:T(8,128)S(1)}, f32[384,768]{1,0:T(8,128)S(1)}) fusion(bf16[197,16,768]{2,1,0:T(8,128)(2,1)S(1)} %slice, bf16[197,16,384]{2,1,0:T(8,128)(2,1)S(1)} %copy-done.6), kind=kOutput, calls=%fused_computation.35 | convolution fusion | flops 1872691200 | bytes 9621504 | tf_op jit(solution)/shard_map/snh,snd->nhd/dot_general | solution.py:27
  126.9 1.4 copy.40
  128.3 1.4 copy.44
  130.4 10.9 %reduce-scatter.13.cloned.1.call-done = f32[192,384]{1,0:T(8,128)} async-done(((f32[768,384]{1,0:T(8,128)}), f32[192,384]{1,0:T(8,128)}) %reduce-scatter.13.cloned.1.call-update) | async-done | bytes 294928
  141.3 1.1 copy.39
  142.5 29.0 %reduce-scatter.17.cloned.1.call-done = f32[192,384]{1,0:T(8,128)} async-done(((f32[768,384]{1,0:T(8,128)}), f32[192,384]{1,0:T(8,128)}) %reduce-scatter.17.cloned.1.call-update) | async-done | bytes 294928
  171.5 1.1 copy.43
  174.5 27.1 %reduce-scatter.15.cloned.1.call-done = f32[192,384]{1,0:T(8,128)} async-done(((f32[768,384]{1,0:T(8,128)}), f32[192,384]{1,0:T(8,128)}) %reduce-scatter.15.cloned.1.call-update) | async-done | bytes 294928
  201.6 1.1 copy.41
  202.7 29.0 %reduce-scatter.19.cloned.1.call-done = f32[192,384]{1,0:T(8,128)} async-done(((f32[768,384]{1,0:T(8,128)}), f32[192,384]{1,0:T(8,128)}) %reduce-scatter.19.cloned.1.call-update) | async-done | bytes 294928
  (41 shorter events, 7.7 us)
Async XLA Ops:
  7.2 43.8 %all-gather.5.cloned.1.call-start = ((), (), s32[]{:S(2)}) async-start(), calls=%async_computation.5 | async-start | bytes 5529600 | tf_op jit(solution)/shard_map/all_gather | solution.py:31
  7.9 84.6 %all-gather.3.cloned.1.call-start = ((), (), s32[]{:S(2)}) async-start(), calls=%async_computation.4 | async-start | bytes 5529600 | tf_op jit(solution)/shard_map/all_gather | solution.py:24
  8.6 132.7 %reduce-scatter.13.cloned.1.call-start = ((), (), s32[]{:S(2)}) async-start(), calls=%async_computation.6 | async-start | bytes 1474560
  92.5 6.1 %copy-start.5 = (f32[197,16,384]{2,1,0:T(8,128)S(1)}, f32[197,16,384]{2,1,0:T(8,128)}, u32[]{:S(2)}) copy-start(f32[197,16,384]{2,1,0:T(8,128)} %get-tuple-element.21) | copy-start | bytes 14524420
  92.5 11.5 %slice-start = ((s8[4841472]{0:T(1024)(128)(4,1)}), s8[4194304]{0:T(1024)(128)(4,1)S(1)}, s32[]{:S(2)}) async-start(s8[4841472]{0:T(1024)(128)(4,1)} %bitcast.31), calls=%async_computation.10 | async-start | bytes 8388608
  96.5 2.2 copy-start
  98.7 5.4 %slice-start.1 = ((s8[4841472]{0:T(1024)(128)(4,1)}), s8[647168]{0:T(1024)(128)(4,1)S(1)}, s32[]{:S(2)}) async-start(s8[4841472]{0:T(1024)(128)(4,1)} %bitcast.31), calls=%async_computation.11 | async-start | bytes 1294336
  113.7 57.7 %reduce-scatter.17.cloned.1.call-start = ((), (), s32[]{:S(2)}) async-start(), calls=%async_computation.8 | async-start | bytes 1474560
  115.2 86.4 %reduce-scatter.15.cloned.1.call-start = ((), (), s32[]{:S(2)}) async-start(), calls=%async_computation.7 | async-start | bytes 1474560
  115.5 3.1 %copy-start.6 = (bf16[197,16,384]{2,1,0:T(8,128)(2,1)S(1)}, bf16[197,16,384]{2,1,0:T(8,128)(2,1)}, u32[]{:S(2)}) copy-start(bf16[197,16,384]{2,1,0:T(8,128)(2,1)} %get-tuple-element.20) | copy-start | bytes 7262212
  126.8 2.9 %copy-start.1 = (bf16[192,384]{1,0:T(8,128)(2,1)S(1)}, bf16[192,384]{1,0:T(8,128)(2,1)}, u32[]{:S(2)}) copy-start(bf16[192,384]{1,0:T(8,128)(2,1)} %param.8) | copy-start | bytes 442372
  126.8 3.1 %copy-start.2 = (bf16[384,192]{0,1:T(8,128)(2,1)S(1)}, bf16[384,192]{0,1:T(8,128)(2,1)}, u32[]{:S(2)}) copy-start(bf16[384,192]{0,1:T(8,128)(2,1)} %param.9) | copy-start | bytes 442372
  126.8 3.2 %copy-start.3 = (f32[192,384]{1,0:T(8,128)S(1)}, f32[192,384]{1,0:T(8,128)}, u32[]{:S(2)}) copy-start(f32[192,384]{1,0:T(8,128)} %param.10) | copy-start | bytes 884740
  126.8 3.4 %copy-start.4 = (f32[384,192]{0,1:T(8,128)S(1)}, f32[384,192]{0,1:T(8,128)}, u32[]{:S(2)}) copy-start(f32[384,192]{0,1:T(8,128)} %param.11) | copy-start | bytes 884740
  128.3 103.4 %reduce-scatter.19.cloned.1.call-start = ((), (), s32[]{:S(2)}) async-start(), calls=%async_computation.9 | async-start | bytes 1474560
Sparse Core Ops, SparseCore 0:
  9.9 41.0 all-gather.4
  52.9 39.5 all-gather.2
  113.9 27.4 reduce-scatter.12
  143.5 27.9 reduce-scatter.16
  173.6 27.9 reduce-scatter.14
  203.8 27.9 reduce-scatter.18
where the time goes:
time: 245 us; the launch traced here: 242 us
  waiting for transfers between devices  144 us (59%)
  local copies, waits for them, and re-layouts  29.7 us (12%)
  matrix products  27.4 us (11%)
  blocking collectives  25.6 us (10%)
  between operations  14.3 us (6%)
    unnamed x10, waiting for transfers between devices  97.4 us
    all_gather x1, waiting for transfers between devices, per_device(): cot_whole = lax.all_gather(cotangent, 'mp', axis=1, tiled=True)  29.6 us
    unnamed x36, local copies, waits for them, and re-layouts  24.4 us
    all_gather x1, waiting for transfers between devices, per_device(): lax.all_gather(inputs, 'mp', axis=1, tiled=True).reshape(SEQ, images, D)  16.7 us
    all_gather x1, blocking collectives, per_device(): lax.all_gather(w_in, 'dp', axis=0, tiled=True)  13.8 us
    all_gather x1, blocking collectives, per_device(): lax.all_gather(w_out, 'dp', axis=1, tiled=True)  11.8 us
    dot_general x1, matrix products, per_device(): jnp.einsum('snh,snd->nhd', act, cot3, preferred_element_type=jnp.float32)  8.2 us
    dot_general x1, matrix products, per_device(): jnp.einsum('snd,snh->ndh', rows_again, delta, preferred_element_type=jnp....  8.2 us
  transfers between devices with their start and end apart: 6, of which 6 were waited for; matrix products, arithmetic and copies ran while one was open for 14% of the time, Pallas kernels for 0%

commit v1 on v0

--- a/solution.py
+++ b/solution.py
@@ -1,10 +1,10 @@
+import functools
 import jax
 import jax.numpy as jnp
 from jax import lax
+from jax.experimental import pallas as pl
+from jax.experimental.pallas import tpu as pltpu
 from jax.sharding import PartitionSpec as P
-
-D = 768
-SEQ = 197
 
 
 def gelu_tanh(v):
@@ -12,6 +12,8 @@
 
 
 def per_device(inputs, cotangent, w_in, w_out, prec_in, prec_out):
+    SEQ = inputs.shape[0]
+    D = w_in.shape[0] * lax.axis_size("dp")
     w_in_full, w_out_full = (
         lax.all_gather(w_in, "dp", axis=0, tiled=True),
         lax.all_gather(w_out, "dp", axis=1, tiled=True),
@@ -50,6 +52,367 @@
     return (new_prec_in, new_prec_out, new_w_in, new_w_out)
 
 
+F32, BF16 = jnp.float32, jnp.bfloat16
+NT = (((1,), (1,)), ((), ()))
+MESH = pl.DeviceIdType.MESH
+
+
+def dot(a, b):
+    return jnp.dot(a, b, preferred_element_type=F32)
+
+
+def dot_nt(a, b):
+    return lax.dot_general(a, b, NT, preferred_element_type=F32)
+
+
+def kernel(
+    x_hbm, c_hbm, win_ref, wout_t_ref, wout_ref, pin_ref, pout_ref,
+    o_pin, o_pout, o_win, o_wout,
+    xg, cg, wg_in, wg_out, w_in_t, w_out_f, act, slope, back, delta,
+    acc, own, stage, recv,
+    loc, ici_s, ici_r, d2d_s, d2d_r, w_s, w_r, rs_s, rs_r,
+):
+    z, m = lax.axis_index("dp"), lax.axis_index("mp")
+    core, q = lax.rem(m, 2), m // 2
+    xx, yy = lax.rem(q, 2), q // 2
+    chips = [yy * 2 + xx, yy * 2 + 1 - xx, (1 - yy) * 2 + xx, (1 - yy) * 2 + 1 - xx]
+    same = [2 * chip + core for chip in chips]
+    other = [2 * chip + 1 - core for chip in chips]
+    xn, yn, partner_id = same[1], same[2], other[0]
+    depth = win_ref.shape[0]
+    width = 4 * depth
+    lo = -(-depth // 128) * 128
+    hi = 3 * depth // 128 * 128
+    ranges = ((0, lo), (hi, width), (lo, hi))
+    images = xg.shape[0]
+
+    def view(p, mm):
+        if p < 2:
+            return xg.at[2 * mm + p]
+        left, right = ranges[(p - 2) // 2]
+        return cg.at[2 * mm + (p - 2) % 2, :, pl.ds(left, right - left)]
+
+    def remote(p, mm, to, ssem, rsem):
+        return pltpu.make_async_remote_copy(
+            src_ref=view(p, mm), dst_ref=view(p, mm), send_sem=ssem, recv_sem=rsem,
+            device_id=(z, to), device_id_type=MESH,
+        )
+
+    def to_x(p):
+        return remote(p, m, xn, ici_s.at[p, 0], ici_r.at[p, 0])
+
+    def to_y(p):
+        return remote(p, m, yn, ici_s.at[p, 1], ici_r.at[p, 1])
+
+    def relayed(p):
+        first = p % 2 == 0
+        return remote(p, same[1 if first else 2], yn if first else xn, ici_s.at[p, 2], ici_r.at[p, 2])
+
+    def across(p, s):
+        return remote(p, same[s], partner_id, d2d_s.at[p, s], d2d_r.at[p, s])
+
+    def arrived(p, s):
+        remote(p, same[s], xn, ici_s.at[p, 0], ici_r.at[p, s - 1]).wait_recv()
+
+    def from_partner(pieces, s):
+        for p in pieces:
+            remote(p, other[s], partner_id, d2d_s.at[p, s], d2d_r.at[p, s]).wait_recv()
+
+    def own_sends(even, odd):
+        for a, b in ((even, odd),):
+            for p in a:
+                to_x(p).start()
+            for p in b:
+                to_y(p).start()
+            for p in b:
+                to_x(p).start()
+            for p in a:
+                to_y(p).start()
+
+    def relay(even, odd):
+        for p in even:
+            arrived(p, 1)
+            relayed(p).start()
+        for p in odd:
+            arrived(p, 2)
+            relayed(p).start()
+        for p in even:
+            across(p, 1).start()
+        for p in odd:
+            across(p, 2).start()
+
+    def second(even, odd):
+        for p in odd:
+            arrived(p, 1)
+            across(p, 1).start()
+        for p in even:
+            arrived(p, 2)
+            across(p, 2).start()
+
+    def third(even, odd):
+        for p in even + odd:
+            arrived(p, 3)
+            across(p, 3).start()
+
+    x_even, x_odd = [0], [1]
+    a_even, a_odd = [2, 4], [3, 5]
+    b_even, b_odd = [6], [7]
+
+    locals_ = []
+    for i in range(2):
+        cols = pl.ds(i * width, width)
+        locals_.append(pltpu.make_async_copy(x_hbm.at[:, cols], xg.at[2 * m + i], loc.at[i]))
+    for i in range(2):
+        cols = pl.ds(i * width, width)
+        locals_.append(pltpu.make_async_copy(c_hbm.at[:, cols], cg.at[2 * m + i], loc.at[2 + i]))
+    for copy in locals_:
+        copy.start()
+
+    barrier = pltpu.get_barrier_semaphore()
+    zs = [lax.rem(z + o, 4) for o in (1, 2, 3)]
+    peers = [(z, xn), (z, yn), (z, partner_id)] + [(there, m) for there in zs]
+    for peer in peers:
+        pl.semaphore_signal(barrier, inc=1, device_id=peer, device_id_type=MESH)
+    pl.semaphore_wait(barrier, len(peers))
+
+    locals_[0].wait()
+    locals_[1].wait()
+    own_sends(x_even, x_odd)
+    for p in x_even + x_odd:
+        across(p, 0).start()
+
+    rows = pl.ds(pl.multiple_of(z * depth, 16), depth)
+
+    def weight(k, o):
+        src, dst = ((win_ref, wg_in), (wout_t_ref, wg_out))[k]
+        return pltpu.make_async_remote_copy(
+            src_ref=src, dst_ref=dst.at[rows], send_sem=w_s.at[k, o], recv_sem=w_r.at[k, o],
+            device_id=(zs[o], m), device_id_type=MESH,
+        )
+
+    for k in range(2):
+        for o in range(3):
+            weight(k, o).start()
+    locals_[2].wait()
+    locals_[3].wait()
+    for p in a_even + a_odd + b_even + b_odd:
+        across(p, 0).start()
+    wg_in[rows, :] = win_ref[...]
+    wg_out[rows, :] = wout_t_ref[...]
+    acc[...] = jnp.zeros_like(acc)
+
+    def forward(chip):
+        def one(j, carry):
+            n = 4 * chip + j
+            pre = dot_nt(w_in_t[...], xg[n])
+            square = pre * pre
+            t = jnp.tanh(0.7978845608028654 * pre * (1.0 + 0.044715 * square))
+            half = 0.5 * (1.0 + t)
+            act[n] = (pre * half).astype(BF16)
+            slope[n] = half + 0.5 * pre * (1.0 - t * t) * (0.7978845608028654 * (1.0 + 0.134145 * square))
+            return carry
+        lax.fori_loop(0, 4, one, 0)
+
+    def accumulate(lhs, rhs, first, count, span):
+        cols = slice(*span)
+        gs = [dot(lhs[first + j], rhs[first + j, :, cols]) for j in range(count)]
+        total, squares = gs[0], gs[0] * gs[0]
+        for g in gs[1:]:
+            total, squares = total + g, squares + g * g
+        acc[0, :, cols] += total
+        acc[1, :, cols] += squares
+
+    def chunk_a(chip):
+        def pair(h, carry):
+            first = 4 * chip + 2 * h
+            for j in range(2):
+                n = first + j
+                back[n] = dot_nt(w_out_f[:, 0:lo], cg[n, :, 0:lo]) + dot_nt(w_out_f[:, hi:width], cg[n, :, hi:width])
+            for span in ranges[:2]:
+                accumulate(act, cg, first, 2, span)
+            return carry
+        lax.fori_loop(0, 2, pair, 0)
+
+    def chunk_b(chip):
+        def pair(h, carry):
+            first = 4 * chip + 2 * h
+            for j in range(2):
+                n = first + j
+                whole = back[n] + dot_nt(w_out_f[:, lo:hi], cg[n, :, lo:hi])
+                delta[n] = (whole * slope[n]).astype(BF16)
+            accumulate(act, cg, first, 2, ranges[2])
+            return carry
+        lax.fori_loop(0, 2, pair, 0)
+
+    def settle(part, span):
+        cols = slice(*span)
+        for a in range(2):
+            turned = acc[a, :, cols].T
+            own[part, a, cols, :] = turned
+            stage[part, a, cols, :] = turned.astype(BF16)
+            if part == 0:
+                acc[a, :, cols] = jnp.zeros_like(acc[a, :, cols])
+
+    def reduce_copy(part, j):
+        slot = lax.rem(z - j + 3, 4)
+        return pltpu.make_async_remote_copy(
+            src_ref=stage.at[part, :, pl.ds(j * depth, depth), :], dst_ref=recv.at[part, slot],
+            send_sem=rs_s.at[part, j], recv_sem=rs_r.at[part, slot],
+            device_id=(j, m), device_id_type=MESH,
+        )
+
+    def give(part, targets):
+        for j in targets:
+            @pl.when(z != j)
+            def _():
+                reduce_copy(part, j).start()
+
+    relay(x_even, x_odd)
+    own_sends(a_even, a_odd)
+    for o in range(3):
+        weight(0, o).wait_recv()
+    w_in_t[...] = wg_in[...].astype(F32).T.astype(BF16)
+    from_partner([0, 1], 0)
+    forward(chips[0])
+    second(x_even, x_odd)
+    from_partner([0, 1], 1)
+    forward(chips[1])
+    from_partner([0, 1], 2)
+    forward(chips[2])
+    third(x_even, x_odd)
+    from_partner([0, 1], 3)
+    forward(chips[3])
+
+    for o in range(3):
+        weight(1, o).wait_recv()
+    w_out_f[...] = wg_out[...].astype(F32).T.astype(BF16)
+    pieces = a_even + a_odd
+    relay(a_even, a_odd)
+    own_sends(b_even, b_odd)
+    from_partner(pieces, 0)
+    chunk_a(chips[0])
+    second(a_even, a_odd)
+    from_partner(pieces, 1)
+    chunk_a(chips[1])
+    from_partner(pieces, 2)
+    chunk_a(chips[2])
+    third(a_even, a_odd)
+    relay(b_even, b_odd)
+    from_partner(pieces, 3)
+    chunk_a(chips[3])
+    settle(0, ranges[0])
+    give(0, [0])
+    settle(0, ranges[1])
+    give(0, [3])
+
+    pieces = b_even + b_odd
+    from_partner(pieces, 0)
+    chunk_b(chips[0])
+    second(b_even, b_odd)
+    from_partner(pieces, 1)
+    chunk_b(chips[1])
+    from_partner(pieces, 2)
+    chunk_b(chips[2])
+    third(b_even, b_odd)
+    from_partner(pieces, 3)
+    chunk_b(chips[3])
+    settle(0, ranges[2])
+    give(0, [1, 2])
+
+    for span, targets in zip(ranges, ([0], [3], [1, 2])):
+        def four(k, carry, span=span):
+            accumulate(delta, xg, 4 * k, 4, span)
+            return carry
+        lax.fori_loop(0, images // 4, four, 0)
+        settle(1, span)
+        give(1, targets)
+
+    scale = 1.0 / (images * 4)
+
+    def collected(part):
+        for t in range(3):
+            pltpu.make_async_remote_copy(
+                src_ref=stage.at[part, :, pl.ds(0, depth), :], dst_ref=recv.at[part, t],
+                send_sem=rs_s.at[part, 0], recv_sem=rs_r.at[part, t],
+                device_id=(zs[t], m), device_id_type=MESH,
+            ).wait_recv()
+        found = []
+        for a in range(2):
+            total = own[part, a, rows, :]
+            for t in range(3):
+                total = total + recv[part, t, a].astype(F32)
+            found.append(total)
+        return found
+
+    total, squares = collected(0)
+    prec = 0.6 * pout_ref[...] + 0.4 * squares.T * scale
+    o_pout[...] = prec
+    mean = wout_ref[...].astype(F32)
+    o_wout[...] = mean - (total.T * scale + 0.1 * mean) / (prec + 0.1)
+    total, squares = collected(1)
+    prec = 0.6 * pin_ref[...] + 0.4 * squares * scale
+    o_pin[...] = prec
+    mean = win_ref[...].astype(F32)
+    o_win[...] = mean - (total * scale + 0.1 * mean) / (prec + 0.1)
+
+    for p in range(8):
+        to_x(p).wait_send()
+        to_y(p).wait_send()
+        relayed(p).wait_send()
+        for s in range(4):
+            across(p, s).wait_send()
+    for k in range(2):
+        for o in range(3):
+            weight(k, o).wait_send()
+    for part in range(2):
+        for j in range(4):
+            @pl.when(z != j)
+            def _():
+                reduce_copy(part, j).wait_send()
+
+
+def fused(inputs, cotangent, w_in, w_out, prec_in, prec_out):
+    seq, local = inputs.shape
+    depth, hid = w_in.shape
+    width = 4 * depth
+    images = 8 * local // width
+    vmem, hbm = pl.BlockSpec(memory_space=pltpu.VMEM), pl.BlockSpec(memory_space=pl.ANY)
+    out = [
+        jax.ShapeDtypeStruct(prec_in.shape, F32),
+        jax.ShapeDtypeStruct(prec_out.shape, F32),
+        jax.ShapeDtypeStruct(prec_in.shape, F32),
+        jax.ShapeDtypeStruct(prec_out.shape, F32),
+    ]
+    dma = pltpu.SemaphoreType.DMA
+    return pl.pallas_call(
+        kernel,
+        out_shape=out,
+        in_specs=[hbm, hbm] + [vmem] * 5,
+        out_specs=[vmem] * 4,
+        scratch_shapes=[
+            pltpu.VMEM((images, seq, width), BF16),
+            pltpu.VMEM((images, seq, width), BF16),
+            pltpu.VMEM((width, hid), BF16),
+            pltpu.VMEM((width, hid), BF16),
+            pltpu.VMEM((hid, width), BF16),
+            pltpu.VMEM((hid, width), BF16),
+            pltpu.VMEM((images, hid, seq), BF16),
+            pltpu.VMEM((images, hid, seq), F32),
+            pltpu.VMEM((images, hid, seq), F32),
+            pltpu.VMEM((images, hid, seq), BF16),
+            pltpu.VMEM((2, hid, width), F32),
+            pltpu.VMEM((2, 2, width, hid), F32),
+            pltpu.VMEM((2, 2, width, hid), BF16),
+            pltpu.VMEM((2, 3, 2, depth, hid), BF16),
+            dma((4,)), dma((8, 3)), dma((8, 3)), dma((8, 4)), dma((8, 4)),
+            dma((2, 3)), dma((2, 3)), dma((2, 4)), dma((2, 3)),
+        ],
+        compiler_params=pltpu.CompilerParams(
+            collective_id=0, has_side_effects=True, vmem_limit_bytes=60 * 1024 * 1024
+        ),
+    )(inputs, cotangent, w_in, w_out.T, w_out, prec_in, prec_out)
+
+
 def solution(mesh):
     placed = (
         P(None, ("dp", "mp")),
@@ -59,8 +422,9 @@
         P("dp", "mp"),
         P("mp", "dp"),
     )
+    body = fused if dict(mesh.shape) == {"dp": 4, "mp": 8} else per_device
     return jax.shard_map(
-        per_device,
+        body,
         mesh=mesh,
         in_specs=placed,
         out_specs=(P("dp", "mp"), P("mp", "dp"), P("dp", "mp"), P("mp", "dp")),

time: 245 us -> 107 us (0.44); the launches traced: 242 us -> 107 us
  waiting for transfers between devices: 144 us -> 0 us
  Pallas kernels: 0 us -> 98.9 us
  matrix products: 27.4 us -> 0 us
  blocking collectives: 25.6 us -> 0 us
  local copies, waits for them, and re-layouts: 29.7 us -> 7.34 us
  between operations: 14.3 us -> 0.66 us
    pallas_call x0 -> x1, Pallas kernels: none -> 98.9 us  [fused(): pl.pallas_call(kernel, out_shape=out, in_specs=[hbm, hbm] + [vmem] * 5, o...]
    unnamed x10 -> x0, waiting for transfers between devices: 97.4 us -> none
    all_gather x2 -> x0, waiting for transfers between devices: 46.3 us -> none  [the longest x1 29.6 us: per_device(): cot_whole = lax.all_gather(cotangent, 'mp', axis=1, tiled=True)]
    dot_general x4 -> x0, matrix products: 27.4 us -> none  [the longest x1 8.2 us: per_device(): jnp.einsum('snh,snd->nhd', act, cot3, preferred_element_type=jnp.float32)]
    all_gather x2 -> x0, blocking collectives: 25.6 us -> none  [the longest x1 13.8 us: per_device(): lax.all_gather(w_in, 'dp', axis=0, tiled=True)]
    unnamed x36 -> x12, local copies, waits for them, and re-layouts: 24.4 us -> 4.57 us
    reshape x2 -> x0, local copies, waits for them, and re-layouts: 5.37 us -> none  [the longest x1 2.83 us: per_device(): cot3 = cot_whole.reshape(SEQ, images, D)]
    pallas_call x0 -> x2, local copies, waits for them, and re-layouts: none -> 2.78 us  [fused(): pl.pallas_call(kernel, out_shape=out, in_specs=[hbm, hbm] + [vmem] * 5, o...]
  transfers between devices with their start and end apart: 6 -> 0, of which waited for: 6 -> 0; matrix products, arithmetic and copies ran while one was open for 14% -> 0% of each run, Pallas kernels for 0% -> 0%
where the time goes in v1:
time: 107 us
  Pallas kernels  98.9 us (92%)
  local copies, waits for them, and re-layouts  7.34 us (7%)
    pallas_call x1, Pallas kernels, fused(): pl.pallas_call(kernel, out_shape=out, in_specs=[hbm, hbm] + [vmem] * 5, o...  98.9 us
    unnamed x12, local copies, waits for them, and re-layouts  4.57 us
    pallas_call x2, local copies, waits for them, and re-layouts, fused(): pl.pallas_call(kernel, out_shape=out, in_specs=[hbm, hbm] + [vmem] * 5, o...  2.78 us

profile of v1, /device:TPU:17, one launch (start us, length us, event | category | flops | bytes accessed | tf_op | source)
XLA Modules:
  0.0 106.9 jit_solution(4784112343713449872)
XLA Ops:
  0.6 0.0 copy-start.3
  0.6 1.8 %copy.10.wout_ref = bf16[384,192]{1,0:T(8,128)(2,1)} copy(bf16[384,192]{0,1:T(8,128)(2,1)} %param.9) | data formatting | bytes 294912 | tf_op args[3]
  2.4 0.0 copy-done.3
  2.4 0.9 copy.11.pout_ref
  3.3 98.9 %shard_map.93 = (f32[192,384]{1,0:T(8,128)}, f32[384,192]{1,0:T(8,128)}, f32[192,384]{1,0:T(8,128)}, f32[384,192]{1,0:T(8,128)}) custom-call(bf16[197,1536]{1,0:T(8,128)(2,1)} %x_hbm.1, bf16[197,1536]{1,0:T(8,128)(2,1)} %c_hbm.1, bf16[192,384]{1,0:T(8,128)(2,1)} %win_ref.1, bf16[192,384]{1,0:T(8,128)(2,1)} %bitcast.1, bf16[384,192]{1,0:T(8,128)(2,1)} %copy.10.wout_ref, ...), custom_call_target="tpu_custom_call" | custom-call | tf_op jit(solution)/shard_map/pallas_call | solution.py:387
  102.2 0.0 copy-start
  102.2 1.9 %copy.12 = f32[384,192]{0,1:T(8,128)} copy(f32[384,192]{1,0:T(8,128)} %get-tuple-element.5) | data formatting | bytes 589824 | tf_op jit(solution)/shard_map/pallas_call | solution.py:387
  104.2 0.0 copy-done
  104.2 0.0 copy-start.2
  104.2 0.9 copy.13
  105.0 0.1 copy-done.2
  105.1 0.0 copy-start.1
  105.1 0.7 copy.16
  105.8 0.4 copy-done.1
  106.2 0.7 copy.17
Async XLA Ops:
  0.6 1.8 %copy-start.3 = (f32[384,192]{0,1:T(8,128)S(1)}, f32[384,192]{0,1:T(8,128)}, u32[]{:S(2)}) copy-start(f32[384,192]{0,1:T(8,128)} %param.11) | copy-start | bytes 884740
  102.2 1.9 %copy-start = (f32[384,192]{1,0:T(8,128)S(1)}, f32[384,192]{1,0:T(8,128)}, u32[]{:S(2)}) copy-start(f32[384,192]{1,0:T(8,128)} %get-tuple-element.7) | copy-start | bytes 884740
  104.2 1.0 copy-start.2
  105.1 1.1 copy-start.1

commit v2 on v1

--- a/solution.py
+++ b/solution.py
@@ -66,11 +66,10 @@
 
 
 def kernel(
-    x_hbm, c_hbm, win_ref, wout_t_ref, wout_ref, pin_ref, pout_ref,
-    o_pin, o_pout, o_win, o_wout,
+    x_hbm, c_hbm, win_ref, wout_t_ref, sums_in, sums_out,
     xg, cg, wg_in, wg_out, w_in_t, w_out_f, act, slope, back, delta,
-    acc, own, stage, recv,
-    loc, ici_s, ici_r, d2d_s, d2d_r, w_s, w_r, rs_s, rs_r,
+    acc, own, stage, recv, passing, joined,
+    loc, ici_s, ici_r, d2d_s, d2d_r, w_s, w_r, rs_s, rs_r, pass_r,
 ):
     z, m = lax.axis_index("dp"), lax.axis_index("mp")
     core, q = lax.rem(m, 2), m // 2
@@ -253,19 +252,59 @@
             if part == 0:
                 acc[a, :, cols] = jnp.zeros_like(acc[a, :, cols])
 
-    def reduce_copy(part, j):
-        slot = lax.rem(z - j + 3, 4)
+    def block(part, j):
+        return stage.at[part, :, pl.ds(j * depth, depth), :]
+
+    def place(j):
+        inner = j in (1, 2)
+        return (1 - j, 3, 2, 1 - int(inner)) if j < 2 else (5 - j, 0, 1, 1 - int(inner))
+
+    def near_copy(part, j):
         return pltpu.make_async_remote_copy(
-            src_ref=stage.at[part, :, pl.ds(j * depth, depth), :], dst_ref=recv.at[part, slot],
-            send_sem=rs_s.at[part, j], recv_sem=rs_r.at[part, slot],
+            src_ref=block(part, j), dst_ref=recv.at[part, 0],
+            send_sem=rs_s.at[part, j], recv_sem=rs_r.at[part, 0],
             device_id=(j, m), device_id_type=MESH,
         )
 
+    def pass_copy(part, j):
+        _, _, far_inner, kind = place(j)
+        return pltpu.make_async_remote_copy(
+            src_ref=block(part, j), dst_ref=passing.at[part, kind],
+            send_sem=rs_s.at[part, j], recv_sem=pass_r.at[part, kind],
+            device_id=(far_inner, m), device_id_type=MESH,
+        )
+
+    def joined_copy(part, j):
+        kind = place(j)[3]
+        return pltpu.make_async_remote_copy(
+            src_ref=joined.at[part, kind], dst_ref=recv.at[part, 1],
+            send_sem=rs_s.at[part, j], recv_sem=rs_r.at[part, 1],
+            device_id=(j, m), device_id_type=MESH,
+        )
+
     def give(part, targets):
         for j in targets:
-            @pl.when(z != j)
+            mate, far_end, _, _ = place(j)
+
+            @pl.when(z == mate)
             def _():
-                reduce_copy(part, j).start()
+                near_copy(part, j).start()
+
+            @pl.when(z == far_end)
+            def _():
+                pass_copy(part, j).start()
+
+    def combine(part, targets):
+        for j in targets:
+            _, _, far_inner, kind = place(j)
+
+            @pl.when(z == far_inner)
+            def _():
+                pass_copy(part, j).wait_recv()
+                for a in range(2):
+                    mine = own[part, a, j * depth:(j + 1) * depth, :]
+                    joined[part, kind, a] = (mine + passing[part, kind, a].astype(F32)).astype(BF16)
+                joined_copy(part, j).start()
 
     relay(x_even, x_odd)
     own_sends(a_even, a_odd)
@@ -318,6 +357,7 @@
     chunk_b(chips[3])
     settle(0, ranges[2])
     give(0, [1, 2])
+    combine(0, [0, 3])
 
     for span, targets in zip(ranges, ([0], [3], [1, 2])):
         def four(k, carry, span=span):
@@ -326,34 +366,21 @@
         lax.fori_loop(0, images // 4, four, 0)
         settle(1, span)
         give(1, targets)
-
-    scale = 1.0 / (images * 4)
-
-    def collected(part):
-        for t in range(3):
-            pltpu.make_async_remote_copy(
-                src_ref=stage.at[part, :, pl.ds(0, depth), :], dst_ref=recv.at[part, t],
-                send_sem=rs_s.at[part, 0], recv_sem=rs_r.at[part, t],
-                device_id=(zs[t], m), device_id_type=MESH,
-            ).wait_recv()
-        found = []
+        if span == ranges[0]:
+            combine(0, [1, 2])
+    combine(1, [0, 3, 1, 2])
+
+    def collected(part, sums):
+        near_copy(part, 0).wait_recv()
+        joined_copy(part, 0).wait_recv()
         for a in range(2):
             total = own[part, a, rows, :]
-            for t in range(3):
+            for t in range(2):
                 total = total + recv[part, t, a].astype(F32)
-            found.append(total)
-        return found
-
-    total, squares = collected(0)
-    prec = 0.6 * pout_ref[...] + 0.4 * squares.T * scale
-    o_pout[...] = prec
-    mean = wout_ref[...].astype(F32)
-    o_wout[...] = mean - (total.T * scale + 0.1 * mean) / (prec + 0.1)
-    total, squares = collected(1)
-    prec = 0.6 * pin_ref[...] + 0.4 * squares * scale
-    o_pin[...] = prec
-    mean = win_ref[...].astype(F32)
-    o_win[...] = mean - (total * scale + 0.1 * mean) / (prec + 0.1)
+            sums[a] = total
+
+    collected(0, sums_out)
+    collected(1, sums_in)
 
     for p in range(8):
         to_x(p).wait_send()
@@ -368,7 +395,7 @@
         for j in range(4):
             @pl.when(z != j)
             def _():
-                reduce_copy(part, j).wait_send()
+                near_copy(part, j).wait_send()
 
 
 def fused(inputs, cotangent, w_in, w_out, prec_in, prec_out):
@@ -377,18 +404,12 @@
     width = 4 * depth
     images = 8 * local // width
     vmem, hbm = pl.BlockSpec(memory_space=pltpu.VMEM), pl.BlockSpec(memory_space=pl.ANY)
-    out = [
-        jax.ShapeDtypeStruct(prec_in.shape, F32),
-        jax.ShapeDtypeStruct(prec_out.shape, F32),
-        jax.ShapeDtypeStruct(prec_in.shape, F32),
-        jax.ShapeDtypeStruct(prec_out.shape, F32),
-    ]
     dma = pltpu.SemaphoreType.DMA
-    return pl.pallas_call(
+    sums_in, sums_out = pl.pallas_call(
         kernel,
-        out_shape=out,
-        in_specs=[hbm, hbm] + [vmem] * 5,
-        out_specs=[vmem] * 4,
+        out_shape=[jax.ShapeDtypeStruct((2, depth, hid), F32)] * 2,
+        in_specs=[hbm, hbm] + [vmem] * 2,
+        out_specs=[vmem] * 2,
         scratch_shapes=[
             pltpu.VMEM((images, seq, width), BF16),
             pltpu.VMEM((images, seq, width), BF16),
@@ -403,14 +424,27 @@
             pltpu.VMEM((2, hid, width), F32),
             pltpu.VMEM((2, 2, width, hid), F32),
             pltpu.VMEM((2, 2, width, hid), BF16),
-            pltpu.VMEM((2, 3, 2, depth, hid), BF16),
+            pltpu.VMEM((2, 2, 2, depth, hid), BF16),
+            pltpu.VMEM((2, 2, 2, depth, hid), BF16),
+            pltpu.VMEM((2, 2, 2, depth, hid), BF16),
             dma((4,)), dma((8, 3)), dma((8, 3)), dma((8, 4)), dma((8, 4)),
-            dma((2, 3)), dma((2, 3)), dma((2, 4)), dma((2, 3)),
+            dma((2, 3)), dma((2, 3)), dma((2, 4)), dma((2, 2)), dma((2, 2)),
         ],
         compiler_params=pltpu.CompilerParams(
             collective_id=0, has_side_effects=True, vmem_limit_bytes=60 * 1024 * 1024
         ),
-    )(inputs, cotangent, w_in, w_out.T, w_out, prec_in, prec_out)
+    )(inputs, cotangent, w_in, w_out.T)
+
+    scale = 1.0 / (images * 4)
+
+    def updated(sums, prec, w):
+        new_prec = 0.6 * prec + 0.4 * sums[1] * scale
+        mean = w.astype(F32)
+        return new_prec, mean - 1.0 * (sums[0] * scale + 0.1 * mean) / (new_prec + 0.1)
+
+    new_prec_in, new_w_in = updated(sums_in, prec_in, w_in)
+    new_prec_out, new_w_out = updated(sums_out, prec_out.T, w_out.T)
+    return new_prec_in, new_prec_out.T, new_w_in, new_w_out.T
 
 
 def solution(mesh):

time: 107 us -> 96.1 us (0.90)
  local copies, waits for them, and re-layouts: 7.34 us -> 0.02 us
  Pallas kernels: 98.9 us -> 91.9 us
  other arithmetic: 0 us -> 2.35 us
    pallas_call x1, Pallas kernels: 98.9 us -> 91.9 us  [fused(): pl.pallas_call(kernel, out_shape=[jax.ShapeDtypeStruct((2, depth, hid), F...]
    unnamed x12 -> x8, local copies, waits for them, and re-layouts: 4.57 us -> 0.02 us
    pallas_call x2 -> x0, local copies, waits for them, and re-layouts: 2.78 us -> none  [fused(): pl.pallas_call(kernel, out_shape=out, in_specs=[hbm, hbm] + [vmem] * 5, o...]
    sub x0 -> x1, other arithmetic: none -> 2.35 us  [updated(): mean - 1.0 * (sums[0] * scale + 0.1 * mean) / (new_prec + 0.1)]
where the time goes in v2:
time: 96.1 us; the launch traced here: 95 us
  Pallas kernels  91.9 us (96%)
  other arithmetic  2.35 us (2%)
    pallas_call x1, Pallas kernels, fused(): pl.pallas_call(kernel, out_shape=[jax.ShapeDtypeStruct((2, depth, hid), F...  91.9 us
    sub x1, other arithmetic, updated(): mean - 1.0 * (sums[0] * scale + 0.1 * mean) / (new_prec + 0.1)  2.35 us

profile of v2, /device:TPU:17, one launch (start us, length us, event | category | flops | bytes accessed | tf_op | source)
XLA Modules:
  0.0 95.0 jit_solution(6279083276622509704)
XLA Ops:
  0.6 0.0 copy-start
  0.6 0.0 copy-start.1
  0.7 0.0 copy-start.2
  0.7 0.0 copy-start.3
  0.7 91.9 %shard_map.93 = (f32[2,192,384]{2,1,0:T(8,128)}, f32[2,192,384]{2,1,0:T(8,128)}) custom-call(bf16[197,1536]{1,0:T(8,128)(2,1)} %x_hbm.1, bf16[197,1536]{1,0:T(8,128)(2,1)} %c_hbm.1, bf16[192,384]{1,0:T(8,128)(2,1)} %win_ref.1, bf16[192,384]{1,0:T(8,128)(2,1)} %bitcast.25), custom_call_target="tpu_custom_call" | custom-call | tf_op jit(solution)/shard_map/pallas_call | solution.py:408
  92.6 0.0 copy-done
  92.6 0.0 copy-done.1
  92.6 0.0 copy-done.2
  92.6 0.0 copy-done.3
  92.6 2.3 %convert_subtract_fusion.1 = (f32[192,384]{1,0:T(8,128)}, f32[192,384]{1,0:T(8,128)}, f32[384,192]{0,1:T(8,128)}, f32[384,192]{0,1:T(8,128)}) fusion(bf16[192,384]{1,0:T(8,128)(2,1)S(1)} %copy-done, f32[2,192,384]{2,1,0:T(8,128)} %get-tuple-element.6, f32[192,384]{1,0:T(8,128)S(1)} %copy-done.2, f32[2,192,384]{2,1,0:T(8,128)} %get-tuple-element.7, ...), kind=kLoop, calls=%fused_computation.2 | loop fusion | flops 1474560 | bytes 3244032 | tf_op jit(solution)/shard_map/sub | solution.py:443
Async XLA Ops:
  0.6 91.9 %copy-start = (bf16[192,384]{1,0:T(8,128)(2,1)S(1)}, bf16[192,384]{1,0:T(8,128)(2,1)}, u32[]{:S(2)}) copy-start(bf16[192,384]{1,0:T(8,128)(2,1)} %win_ref.1) | copy-start | bytes 442372
  0.6 91.9 %copy-start.1 = (bf16[384,192]{0,1:T(8,128)(2,1)S(1)}, bf16[384,192]{0,1:T(8,128)(2,1)}, u32[]{:S(2)}) copy-start(bf16[384,192]{0,1:T(8,128)(2,1)} %param.9) | copy-start | bytes 442372
  0.7 91.9 %copy-start.2 = (f32[192,384]{1,0:T(8,128)S(1)}, f32[192,384]{1,0:T(8,128)}, u32[]{:S(2)}) copy-start(f32[192,384]{1,0:T(8,128)} %param.10) | copy-start | bytes 884740
  0.7 91.9 %copy-start.3 = (f32[384,192]{0,1:T(8,128)S(1)}, f32[384,192]{0,1:T(8,128)}, u32[]{:S(2)}) copy-start(f32[384,192]{0,1:T(8,128)} %param.11) | copy-start | bytes 884740
